TPU v7x, 32 devices: a whole 2x2x4 slice. The times are simulated.
32 devices in a mesh: dp: 4 (over y, x), tensor: 8 (over z, core).
Axes of the slice: x: 2, y: 2, z: 4, core: 2. Of those that a mesh axis runs over, the one named last changes fastest.
Arguments:
- queries: bfloat16 [1536, 8192], P('dp', 'tensor'), may hold values from -180 to 180
- keys: bfloat16 [1536, 1024], P('dp'), may hold values from -4.5 to 4.5
- values: bfloat16 [1536, 1024], P('dp'), may hold values from -6 to 6
- grad_out: bfloat16 [1536, 8192], P('dp', 'tensor'), may hold values from -3 to 3
- weight: float32 [8192, 8192], P('dp', 'tensor'), as said below
- first_code: bfloat16 [8192, 8192], P('dp', 'tensor'), may hold values from -1 to 1, as said below
- first_rows: float32 [8192], P('dp'), may hold values from 0.2 to 5
- first_cols: float32 [8192], P('tensor'), may hold values from 0.2 to 5
- second_code: bfloat16 [8192, 8192], P('dp', 'tensor'), may hold values from 0 to 1, as said below
- second_rows: float32 [8192], P('dp'), may hold values from 0.5 to 20
- second_cols: float32 [8192], P('tensor'), may hold values from 0.5 to 20
Outputs:
- grad_queries: bfloat16 [1536, 8192], P('dp', 'tensor')
- new_weight: float32 [8192, 8192], P('dp', 'tensor')
- next_first_code: bfloat16 [8192, 8192], P('dp', 'tensor')
- next_first_rows: float32 [8192], P('dp')
- next_first_cols: float32 [8192], P('tensor')
- next_second_code: bfloat16 [8192, 8192], P('dp', 'tensor')
- next_second_rows: float32 [8192], P('dp')
- next_second_cols: float32 [8192], P('tensor')
Inputs may be any that keep to these rules, and one draw needn't show every extreme that they name: `weight`: rows 8192 onward are zero. `first_code`: rows 8192 onward are zero. `second_code`: rows 8192 onward are zero; all other entries are 0.05 or more.
All inputs are finite; a program needn't handle non-finite values.
Results may differ from a plain program's by a relative error of at most 0.023.
Values may be sent and summed in bfloat16 or wider, within the bound.
A program may use at most 128 MiB of HBM per device.

v0:
```python
import jax
import jax.numpy as jnp
from jax import lax
from jax.sharding import PartitionSpec as P

H = 64
KVH = 8
HD = 128
beta_first = 0.9
beta_second = 0.95
learning = 0.01
decay_rate = 0.1
adam_eps = 1e-08
code_eps = 1e-06
correct_first = 1.0 - 0.9**10
correct_second = 1.0 - 0.95**10


def attend(queries, key_sel, value_sel, heads_dev):
    length = queries.shape[0]
    query_heads = queries.reshape(length, heads_dev, HD)
    scores = jnp.einsum(
        "qhd,kd->hqk", query_heads, key_sel, preferred_element_type=jnp.float32
    ) * HD ** (-0.5)
    future = lax.broadcasted_iota(jnp.int32, (length, length), 1) > lax.broadcasted_iota(
        jnp.int32, (length, length), 0
    )
    scores = jnp.where(future[None], -1e30, scores)
    highest = jnp.max(scores, axis=-1, keepdims=True)
    exponent = jnp.exp(scores - highest)
    probabilities = exponent / jnp.sum(exponent, axis=-1, keepdims=True)
    weights_half = probabilities.astype(jnp.bfloat16)
    attended = jnp.einsum(
        "hqk,kd->qhd", weights_half, value_sel, preferred_element_type=jnp.float32
    )
    return (probabilities, attended.astype(jnp.bfloat16).reshape(length, heads_dev * HD))


def attend_back(probabilities, attended, grad_half, key_sel, value_sel, heads_dev):
    length = grad_half.shape[0]
    grad_heads = grad_half.reshape(length, heads_dev, HD)
    grad_probs = jnp.einsum(
        "qhd,kd->hqk", grad_heads, value_sel, preferred_element_type=jnp.float32
    )
    row_dot = jnp.sum(
        grad_heads.astype(jnp.float32)
        * attended.reshape(length, heads_dev, HD).astype(jnp.float32),
        axis=-1,
    )
    grad_scores = (probabilities * (grad_probs - row_dot.T[:, :, None])).astype(jnp.bfloat16)
    grad_query = jnp.einsum(
        "hqk,kd->qhd", grad_scores, key_sel, preferred_element_type=jnp.float32
    ) * HD ** (-0.5)
    return grad_query.astype(jnp.bfloat16).reshape(length, heads_dev * HD)


def per_device(
    queries,
    keys,
    values,
    grad_out,
    weight,
    first_code,
    first_rows,
    first_cols,
    second_code,
    second_rows,
    second_cols,
):
    dp_count = lax.axis_size("dp")
    cols_dev = queries.shape[1]
    heads_dev = cols_dev // HD
    rows_dev = weight.shape[0]
    width_pad = dp_count * rows_dev
    tensor_index = lax.axis_index("tensor")
    kv_start = tensor_index * heads_dev // (H // KVH) * HD
    weight_half = weight.astype(jnp.bfloat16)
    full_grad = lax.all_gather(grad_out, "tensor", axis=1, tiled=True)
    padded = jnp.pad(full_grad, ((0, 0), (0, width_pad - full_grad.shape[1])))
    key_sel = lax.dynamic_slice_in_dim(keys, kv_start, HD, 1)
    value_sel = lax.dynamic_slice_in_dim(values, kv_start, HD, 1)
    probabilities, attended = attend(queries, key_sel, value_sel, heads_dev)
    block = padded
    grad_att = jnp.dot(
        block,
        lax.all_gather(weight_half, "dp", axis=0, tiled=True),
        preferred_element_type=jnp.float32,
    )
    block = padded
    weight_grad = lax.psum_scatter(
        jnp.einsum("sc,sh->ch", block, attended, preferred_element_type=jnp.float32).astype(
            jnp.bfloat16
        ),
        "dp",
        scatter_dimension=0,
        tiled=True,
    ).astype(jnp.float32)
    grad_half = grad_att.astype(jnp.bfloat16)
    grad_queries = attend_back(probabilities, attended, grad_half, key_sel, value_sel, heads_dev)
    first = first_code.astype(jnp.float32) * jnp.minimum(first_rows[:, None], first_cols[None, :])
    second = second_code.astype(jnp.float32) * jnp.minimum(
        second_rows[:, None], second_cols[None, :]
    )
    first_new = beta_first * first + (1.0 - beta_first) * weight_grad
    second_new = beta_second * second + (1.0 - beta_second) * weight_grad * weight_grad
    step_size = first_new / correct_first / (jnp.sqrt(second_new / correct_second) + adam_eps)
    new_weight = weight - learning * (step_size + decay_rate * weight)
    first_abs = jnp.abs(first_new)
    second_abs = jnp.abs(second_new)
    local_rows_max = jnp.stack([jnp.max(first_abs, axis=1), jnp.max(second_abs, axis=1)])
    local_cols_max = jnp.stack([jnp.max(first_abs, axis=0), jnp.max(second_abs, axis=0)])
    rows_mine = lax.pmax(local_rows_max, "tensor")
    cols_mine = lax.pmax(local_cols_max, "dp")
    next_first_code = (
        first_new / (jnp.minimum(rows_mine[0][:, None], cols_mine[0][None, :]) + code_eps)
    ).astype(jnp.bfloat16)
    next_second_code = (
        second_new / (jnp.minimum(rows_mine[1][:, None], cols_mine[1][None, :]) + code_eps)
    ).astype(jnp.bfloat16)
    return (
        grad_queries,
        new_weight,
        next_first_code,
        rows_mine[0],
        cols_mine[0],
        next_second_code,
        rows_mine[1],
        cols_mine[1],
    )


def solution(mesh):
    return jax.shard_map(
        per_device,
        mesh=mesh,
        in_specs=(
            P("dp", "tensor"),
            P("dp", None),
            P("dp", None),
            P("dp", "tensor"),
            P("dp", "tensor"),
            P("dp", "tensor"),
            P("dp"),
            P("tensor"),
            P("dp", "tensor"),
            P("dp"),
            P("tensor"),
        ),
        out_specs=(
            P("dp", "tensor"),
            P("dp", "tensor"),
            P("dp", "tensor"),
            P("dp"),
            P("tensor"),
            P("dp", "tensor"),
            P("dp"),
            P("tensor"),
        ),
        check_vma=False,
    )
```

profile of v0, /device:TPU:0, one launch (start us, length us, event | category | flops | bytes accessed | tf_op | source)
XLA Modules:
  0.0 510.6 jit_solution(8589471572485193456)
XLA Ops:
  7.2 0.0 copy-start
  7.2 0.0 all-gather.3.cloned.1.call-start
  7.2 0.7 all-gather.3.cloned.1.call-update
  7.9 0.0 copy-start.1
  7.9 0.0 all-gather.5.cloned.1.call-start
  8.0 6.1 %convert_element_type.51 = bf16[2048,1024]{1,0:T(8,128)(2,1)} convert(f32[2048,1024]{1,0:T(8,128)} %param.15) | non-fusion elementwise | flops 2097152 | bytes 12582912 | tf_op jit(solution)/shard_map/convert_element_type | solution.py:77
  14.1 0.0 all-gather.5.cloned.1.call-update
  14.1 0.0 reduce-scatter.2.cloned.1.call-start
  14.2 0.0 copy-done
  14.3 0.0 copy-done.1
  14.3 0.8 fusion.21
  15.1 3.7 fusion.42
  18.7 58.3 %all-gather.3.cloned.1.call-done = bf16[384,8192]{1,0:T(8,128)(2,1)} async-done(((bf16[384,1024]{1,0:T(8,128)(2,1)}), bf16[384,8192]{1,0:T(8,128)(2,1)}) %all-gather.3.cloned.1.call-update) | async-done | bytes 6291472 | tf_op jit(solution)/shard_map/all_gather | solution.py:78
  77.0 158.4 %all-gather.5.cloned.1.call-done = bf16[8192,1024]{1,0:T(8,128)(2,1)} async-done(((bf16[2048,1024]{1,0:T(8,128)(2,1)}), bf16[8192,1024]{1,0:T(8,128)(2,1)}) %all-gather.5.cloned.1.call-update) | async-done | bytes 16777232 | tf_op jit(solution)/shard_map/all_gather | solution.py:86
  235.4 12.1 %convolution_convert_fusion = bf16[384,1024]{1,0:T(8,128)(2,1)S(1)} fusion(bf16[384,8192]{1,0:T(8,128)(2,1)} %all-gather.3.cloned.1.call-done, bf16[8192,1024]{1,0:T(8,128)(2,1)} %all-gather.5.cloned.1.call-done), kind=kOutput, calls=%fused_computation.30 | convolution fusion | flops 6442844160 | bytes 23855104 | tf_op jit(solution)/shard_map/dot_general | solution.py:84
  247.5 0.4 copy.37
  247.9 3.0 multiply_reduce_fusion
  250.9 14.5 %convert_bitcast_fusion = bf16[8192,1024]{0,1:T(8,128)(2,1)} fusion(bf16[384,1024]{0,1:T(8,128)(2,1)S(1)} %bitcast.82, bf16[384,8192]{1,0:T(8,128)(2,1)} %all-gather.3.cloned.1.call-done), kind=kOutput, calls=%fused_computation.1 | convolution fusion | flops 6450839552 | bytes 23855104 | tf_op jit(solution)/shard_map/sc,sh->ch/dot_general | solution.py:91
  265.4 0.0 reduce-scatter.2.cloned.1.call-update
  265.4 9.4 %copy.28 = f32[2048,1024]{0,1:T(8,128)} copy(f32[2048,1024]{1,0:T(8,128)} %param.15) | data formatting | bytes 16777216 | tf_op args[4]
  274.8 6.4 %copy.25 = bf16[2048,1024]{0,1:T(8,128)(2,1)} copy(bf16[2048,1024]{1,0:T(8,128)(2,1)} %param.16) | data formatting | bytes 8388608 | tf_op args[5]
  281.2 6.5 %copy.26 = bf16[2048,1024]{0,1:T(8,128)(2,1)} copy(bf16[2048,1024]{1,0:T(8,128)(2,1)} %param.19) | data formatting | bytes 8388608 | tf_op args[8]
  287.7 0.0 copy-start.4
  287.7 0.0 copy-start.5
  287.7 0.0 copy-start.8
  287.7 0.0 copy-start.9
  287.7 3.7 multiply_convert_fusion
  291.5 1.2 copy.29
  292.6 126.6 %reduce-scatter.2.cloned.1.call-done = bf16[2048,1024]{0,1:T(8,128)(2,1)} async-done(((bf16[8192,1024]{0,1:T(8,128)(2,1)}), bf16[2048,1024]{0,1:T(8,128)(2,1)}) %reduce-scatter.2.cloned.1.call-update) | async-done | bytes 4194320 | tf_op jit(solution)/shard_map/reduce_scatter | solution.py:90
  419.3 0.0 copy-done.4
  419.3 0.0 copy-done.5
  419.3 0.0 copy-done.8
  419.3 0.0 copy-done.9
  419.3 15.6 %abs_reduce_fusion.3 = (f32[2048]{0:T(1024)S(1)}, f32[1024]{0:T(1024)S(1)}, f32[1024]{0:T(1024)S(1)}, f32[2048]{0:T(1024)S(1)}, f32[2048,1024]{0,1:T(8,128)}) fusion(bf16[2048,1024]{0,1:T(8,128)(2,1)} %reduce-scatter.2.cloned.1.call-done, f32[1024]{0:T(1024)S(1)} %copy-done.8, f32[2048]{0:T(1024)S(1)} %copy-done.4, bf16[2048,1024]{0,1:T(8,128)(2,1)} %copy.25, ...), kind=kLoop, calls=%fused_computation.12 | loop fusion | flops 58714112 | bytes 29409280 | tf_op jit(solution)/shard_map/reduce_max | solution.py:110
  434.9 9.2 %copy.30 = f32[2048,1024]{1,0:T(8,128)} copy(f32[2048,1024]{0,1:T(8,128)} %get-tuple-element.22) | data formatting | bytes 16777216
  444.2 9.1 %pmax.15 = f32[2,1024]{1,0:T(2,128)S(1)} all-reduce(f32[2,1024]{1,0:T(2,128)S(1)} %pad_maximum_fusion.1), channel_id=1, replica_groups=mesh['dp'=4,'tensor'=8] {'dp'}, use_global_device_ids=true, to_apply=%region_9.10 | all-reduce | flops 2048 | bytes 16384 | tf_op jit(solution)/shard_map/pmax | solution.py:113
  453.3 0.0 copy-start.6
  453.3 0.0 copy-start.7
  453.4 26.4 %pmax.14 = f32[2,2048]{1,0:T(2,128)S(1)} all-reduce(f32[2,2048]{1,0:T(2,128)S(1)} %pad_maximum_fusion), channel_id=1, replica_groups=mesh['dp'=4,'tensor'=8] {'tensor'}, use_global_device_ids=true, to_apply=%region_6.7 | all-reduce | flops 4096 | bytes 32768 | tf_op jit(solution)/shard_map/pmax | solution.py:112
  479.7 0.0 copy-start.2
  479.7 0.0 copy-start.3
  479.7 11.5 %divide_convert_fusion = (bf16[2048,1024]{0,1:T(8,128)(2,1)}, bf16[2048,1024]{0,1:T(8,128)(2,1)}) fusion(f32[1024]{0:T(1024)S(1)} %bitcast.76, f32[2048]{0:T(1024)S(1)} %bitcast.70, bf16[2048,1024]{0,1:T(8,128)(2,1)} %reduce-scatter.2.cloned.1.call-done, f32[1024]{0:T(1024)S(1)} %copy-done.9, f32[2048]{0:T(1024)S(1)} %copy-done.5, ...), kind=kLoop, calls=%fused_computation.6 | loop fusion | flops 46137344 | bytes 21020672 | tf_op jit(solution)/shard_map/convert_element_type | solution.py:119
  491.3 0.0 copy-done.6
  491.3 0.0 copy-done.7
  491.3 0.0 copy-done.2
  491.3 0.0 copy-done.3
  491.3 6.4 %copy.31 = bf16[2048,1024]{1,0:T(8,128)(2,1)} copy(bf16[2048,1024]{0,1:T(8,128)(2,1)} %get-tuple-element.24) | data formatting | bytes 8388608
  497.7 6.4 %copy.32 = bf16[2048,1024]{1,0:T(8,128)(2,1)} copy(bf16[2048,1024]{0,1:T(8,128)(2,1)} %get-tuple-element.23) | data formatting | bytes 8388608
  (5 shorter events, 0.1 us)
Async XLA Ops:
  7.2 7.1 %copy-start = (bf16[384,1024]{1,0:T(8,128)(2,1)S(1)}, bf16[384,1024]{1,0:T(8,128)(2,1)}, u32[]{:S(2)}) copy-start(bf16[384,1024]{1,0:T(8,128)(2,1)} %param.12) | copy-start | bytes 2359300
  7.2 69.9 %all-gather.3.cloned.1.call-start = ((), (), s32[]{:S(2)}) async-start(), calls=%async_computation.1 | async-start | bytes 7077888 | tf_op jit(solution)/shard_map/all_gather | solution.py:78
  7.9 6.3 %copy-start.1 = (bf16[384,1024]{1,0:T(8,128)(2,1)S(1)}, bf16[384,1024]{1,0:T(8,128)(2,1)}, u32[]{:S(2)}) copy-start(bf16[384,1024]{1,0:T(8,128)(2,1)} %param.11) | copy-start | bytes 2359300
  7.9 227.5 %all-gather.5.cloned.1.call-start = ((), (), s32[]{:S(2)}) async-start(), calls=%async_computation.2 | async-start | bytes 20971520 | tf_op jit(solution)/shard_map/all_gather | solution.py:86
  14.1 405.2 %reduce-scatter.2.cloned.1.call-start = ((), (), s32[]{:S(2)}) async-start(), calls=%async_computation.3 | async-start | bytes 20971520 | tf_op jit(solution)/shard_map/reduce_scatter | solution.py:90
  287.7 131.6 %copy-start.4 = (f32[2048]{0:T(1024)S(1)}, f32[2048]{0:T(1024)}, u32[]{:S(2)}) copy-start(f32[2048]{0:T(1024)} %param.17) | copy-start | bytes 24580
  287.7 131.6 %copy-start.5 = (f32[2048]{0:T(1024)S(1)}, f32[2048]{0:T(1024)}, u32[]{:S(2)}) copy-start(f32[2048]{0:T(1024)} %param.20) | copy-start | bytes 24580
  287.7 131.6 %copy-start.8 = (f32[1024]{0:T(1024)S(1)}, f32[1024]{0:T(1024)}, u32[]{:S(2)}) copy-start(f32[1024]{0:T(1024)} %param.18) | copy-start | bytes 12292
  287.7 131.6 %copy-start.9 = (f32[1024]{0:T(1024)S(1)}, f32[1024]{0:T(1024)}, u32[]{:S(2)}) copy-start(f32[1024]{0:T(1024)} %param.21) | copy-start | bytes 12292
  453.3 38.0 %copy-start.6 = (f32[1,1024]{1,0:T(1,128)}, f32[1,1024]{1,0:T(1,128)S(1)}, u32[]{:S(2)}) copy-start(f32[1,1024]{1,0:T(1,128)S(1)} %get-tuple-element.27) | copy-start | bytes 12292
  453.3 37.9 %copy-start.7 = (f32[1,1024]{1,0:T(1,128)}, f32[1,1024]{1,0:T(1,128)S(1)}, u32[]{:S(2)}) copy-start(f32[1,1024]{1,0:T(1,128)S(1)} %get-tuple-element.28) | copy-start | bytes 12292
  479.7 11.5 %copy-start.2 = (f32[1,2048]{1,0:T(1,128)}, f32[1,2048]{1,0:T(1,128)S(1)}, u32[]{:S(2)}) copy-start(f32[1,2048]{1,0:T(1,128)S(1)} %get-tuple-element.25) | copy-start | bytes 24580
  479.7 11.5 %copy-start.3 = (f32[1,2048]{1,0:T(1,128)}, f32[1,2048]{1,0:T(1,128)S(1)}, u32[]{:S(2)}) copy-start(f32[1,2048]{1,0:T(1,128)S(1)} %get-tuple-element.26) | copy-start | bytes 24580
Sparse Core Ops, SparseCore 0:
  9.6 67.4 all-gather.2
  79.5 155.9 all-gather.4
  265.5 153.7 reduce-scatter.1
where the time goes:
time: 512 us; the launch traced here: 511 us
  waiting for transfers between devices  344 us (67%)
  local copies, waits for them, and re-layouts  46 us (9%)
  other arithmetic  37 us (7%)
  blocking collectives  35.4 us (7%)
  matrix products  34.1 us (7%)
  between operations  13.9 us (3%)
    all_gather x1, waiting for transfers between devices, per_device(): lax.all_gather(weight_half, 'dp', axis=0, tiled=True)  158 us
    reduce_scatter x1, waiting for transfers between devices, per_device(): lax.psum_scatter(jnp.einsum('sc,sh->ch', block, attended, preferred_eleme...  127 us
    all_gather x1, waiting for transfers between devices, per_device(): full_grad = lax.all_gather(grad_out, 'tensor', axis=1, tiled=True)  58.3 us
    unnamed x27, local copies, waits for them, and re-layouts  45.6 us
    pmax x1, blocking collectives, per_device(): rows_mine = lax.pmax(local_rows_max, 'tensor')  26.4 us
    reduce_max x1, other arithmetic, per_device(): jnp.max(first_abs, axis=1)  15.6 us
    dot_general x1, matrix products, per_device(): jnp.einsum('sc,sh->ch', block, attended, preferred_element_type=jnp.float32)  14.5 us
    dot_general x1, matrix products, per_device(): jnp.dot(block, lax.all_gather(weight_half, 'dp', axis=0, tiled=True), pre...  12.1 us
  transfers between devices with their start and end apart: 3, of which 3 were waited for; matrix products, arithmetic and copies ran while one was open for 7% of the time, Pallas kernels for 0%

commit v1 on v0

--- a/solution.py
+++ b/solution.py
@@ -75,7 +75,14 @@
     tensor_index = lax.axis_index("tensor")
     kv_start = tensor_index * heads_dev // (H // KVH) * HD
     weight_half = weight.astype(jnp.bfloat16)
-    full_grad = lax.all_gather(grad_out, "tensor", axis=1, tiled=True)
+    ring = [grad_out]
+    for hop in range(7):
+        ring.append(lax.ppermute(ring[-1], "tensor", [(dev, (dev + 1) % 8) for dev in range(8)]))
+    full_grad = jnp.roll(
+        jnp.concatenate(ring[::-1], axis=1),
+        (lax.axis_index("tensor") + 1) * ring[0].shape[1],
+        axis=1,
+    )
     padded = jnp.pad(full_grad, ((0, 0), (0, width_pad - full_grad.shape[1])))
     key_sel = lax.dynamic_slice_in_dim(keys, kv_start, HD, 1)
     value_sel = lax.dynamic_slice_in_dim(values, kv_start, HD, 1)

time: 512 us -> 486 us (0.949)
  local copies, waits for them, and re-layouts: 46 us -> 14.7 us
    ppermute x0 -> x7, waiting for transfers between devices: none -> 85.3 us  [per_device(): lax.ppermute(ring[-1], 'tensor', [(dev, (dev + 1) % 8) for dev in range(8)])]
    all_gather x1 -> x0, waiting for transfers between devices: 58.3 us -> none  [per_device(): full_grad = lax.all_gather(grad_out, 'tensor', axis=1, tiled=True)]
    all_gather x1, waiting for transfers between devices: 158 us -> 111 us  [per_device(): lax.all_gather(weight_half, 'dp', axis=0, tiled=True)]
    unnamed x27 -> x46, local copies, waits for them, and re-layouts: 45.6 us -> 14.3 us
    reduce_scatter x1, waiting for transfers between devices: 127 us -> 152 us  [per_device(): lax.psum_scatter(jnp.einsum('sc,sh->ch', block, attended, preferred_eleme...]
    convert_element_type x1 -> x0, other arithmetic: 6.13 us -> none  [per_device(): weight_half = weight.astype(jnp.bfloat16)]
    reduce_max x1, other arithmetic: 15.6 us -> 20.8 us  [per_device(): jnp.max(first_abs, axis=1)]
  transfers between devices with their start and end apart: 3 -> 9, of which waited for: 3 -> 9; matrix products, arithmetic and copies ran while one was open for 7% -> 4% of each run, Pallas kernels for 0% -> 0%
where the time goes in v1:
time: 486 us
  waiting for transfers between devices  348 us (72%)
  matrix products  36.2 us (7%)
  other arithmetic  35.7 us (7%)
  blocking collectives  35.4 us (7%)
  local copies, waits for them, and re-layouts  14.7 us (3%)
  between operations  14.4 us (3%)
    reduce_scatter x1, waiting for transfers between devices, per_device(): lax.psum_scatter(jnp.einsum('sc,sh->ch', block, attended, preferred_eleme...  152 us
    all_gather x1, waiting for transfers between devices, per_device(): lax.all_gather(weight_half, 'dp', axis=0, tiled=True)  111 us
    ppermute x7, waiting for transfers between devices, per_device(): lax.ppermute(ring[-1], 'tensor', [(dev, (dev + 1) % 8) for dev in range(8)])  85.3 us
    pmax x1, blocking collectives, per_device(): rows_mine = lax.pmax(local_rows_max, 'tensor')  26.3 us
    reduce_max x1, other arithmetic, per_device(): jnp.max(first_abs, axis=1)  20.8 us
    dot_general x1, matrix products, per_device(): jnp.einsum('sc,sh->ch', block, attended, preferred_element_type=jnp.float32)  15.3 us
    unnamed x46, local copies, waits for them, and re-layouts  14.3 us
    dot_general x1, matrix products, per_device(): jnp.dot(block, lax.all_gather(weight_half, 'dp', axis=0, tiled=True), pre...  12.2 us
  transfers between devices with their start and end apart: 9, of which 9 were waited for; matrix products, arithmetic and copies ran while one was open for 4% of the time, Pallas kernels for 0%

profile of v1, /device:TPU:0, one launch (start us, length us, event | category | flops | bytes accessed | tf_op | source)
XLA Modules:
  0.0 485.7 jit_solution(14511362511993969023)
XLA Ops:
  7.2 0.0 copy-start
  7.2 0.0 reduce-scatter.2.cloned.1.call-start
  7.2 0.5 collective-permute-start
  7.8 13.9 %collective-permute-done = bf16[384,1024]{1,0:T(8,128)(2,1)S(1)} collective-permute-done((bf16[384,1024]{1,0:T(8,128)(2,1)}, bf16[384,1024]{1,0:T(8,128)(2,1)S(1)}, u32[]{:S(2)}, u32[]{:S(2)}) %collective-permute-start) | collective-permute-done | bytes 786464 | tf_op jit(solution)/shard_map/ppermute | solution.py:80
  21.7 13.2 %collective-permute-done.1 = bf16[384,1024]{1,0:T(8,128)(2,1)S(1)} collective-permute-done((bf16[384,1024]{1,0:T(8,128)(2,1)S(1)}, bf16[384,1024]{1,0:T(8,128)(2,1)S(1)}, u32[]{:S(2)}, u32[]{:S(2)}) %collective-permute-start.1) | collective-permute-done | bytes 786464 | tf_op jit(solution)/shard_map/ppermute | solution.py:80
  34.9 13.2 %collective-permute-done.2 = bf16[384,1024]{1,0:T(8,128)(2,1)S(1)} collective-permute-done((bf16[384,1024]{1,0:T(8,128)(2,1)S(1)}, bf16[384,1024]{1,0:T(8,128)(2,1)S(1)}, u32[]{:S(2)}, u32[]{:S(2)}) %collective-permute-start.2) | collective-permute-done | bytes 786464 | tf_op jit(solution)/shard_map/ppermute | solution.py:80
  48.1 13.2 %collective-permute-done.3 = bf16[384,1024]{1,0:T(8,128)(2,1)S(1)} collective-permute-done((bf16[384,1024]{1,0:T(8,128)(2,1)S(1)}, bf16[384,1024]{1,0:T(8,128)(2,1)S(1)}, u32[]{:S(2)}, u32[]{:S(2)}) %collective-permute-start.3) | collective-permute-done | bytes 786464 | tf_op jit(solution)/shard_map/ppermute | solution.py:80
  61.3 0.9 copy-done.2
  62.2 13.3 %collective-permute-done.4 = bf16[384,1024]{1,0:T(8,128)(2,1)} collective-permute-done((bf16[384,1024]{1,0:T(8,128)(2,1)S(1)}, bf16[384,1024]{1,0:T(8,128)(2,1)}, u32[]{:S(2)}, u32[]{:S(2)}) %collective-permute-start.4) | collective-permute-done | bytes 786464 | tf_op jit(solution)/shard_map/ppermute | solution.py:80
  75.6 1.9 fusion.27
  77.5 11.5 %collective-permute-done.5 = bf16[384,1024]{1,0:T(8,128)(2,1)} collective-permute-done((bf16[384,1024]{1,0:T(8,128)(2,1)}, bf16[384,1024]{1,0:T(8,128)(2,1)}, u32[]{:S(2)}, u32[]{:S(2)}) %collective-permute-start.5) | collective-permute-done | bytes 786464 | tf_op jit(solution)/shard_map/ppermute | solution.py:80
  89.1 3.6 fusion.50
  92.6 3.1 fusion.21
  95.7 6.8 %collective-permute-done.6 = bf16[384,1024]{1,0:T(8,128)(2,1)} collective-permute-done((bf16[384,1024]{1,0:T(8,128)(2,1)}, bf16[384,1024]{1,0:T(8,128)(2,1)}, u32[]{:S(2)}, u32[]{:S(2)}) %collective-permute-start.6) | collective-permute-done | bytes 786464 | tf_op jit(solution)/shard_map/ppermute | solution.py:80
  102.6 1.2 constant_dynamic-update-slice_fusion.15
  103.8 1.2 constant_dynamic-update-slice_fusion.14
  105.0 1.2 constant_dynamic-update-slice_fusion.13
  106.2 0.1 constant_dynamic-update-slice_fusion.12
  106.2 0.1 constant_dynamic-update-slice_fusion.11
  106.3 0.1 constant_dynamic-update-slice_fusion.10
  106.3 0.1 constant_dynamic-update-slice_fusion.9
  106.4 0.1 constant_dynamic-update-slice_fusion.8
  106.5 1.2 constant_dynamic-update-slice_fusion.7
  107.7 1.2 constant_dynamic-update-slice_fusion.6
  108.9 1.2 constant_dynamic-update-slice_fusion.5
  110.0 0.1 constant_dynamic-update-slice_fusion.4
  110.1 0.1 constant_dynamic-update-slice_fusion.3
  110.2 0.1 constant_dynamic-update-slice_fusion.2
  110.2 0.1 constant_dynamic-update-slice_fusion.1
  110.3 0.1 constant_dynamic-update-slice_fusion
  110.4 4.5 copy-done.6
  114.9 15.3 %convolution_convert_fusion = bf16[8192,1024]{1,0:T(8,128)(2,1)} fusion(bf16[384,1024]{0,1:T(8,128)(2,1)S(1)} %bitcast.63, bf16[384,16384]{1,0:T(8,128)(2,1)} %copy-done.6, s32[]{:T(128)S(6)} %select_n.29), kind=kOutput, calls=%fused_computation.1 | convolution fusion | flops 6450839552 | bytes 23855108 | tf_op jit(solution)/shard_map/sc,sh->ch/dot_general | solution.py:98
  130.3 0.0 reduce-scatter.2.cloned.1.call-update
  130.3 0.2 all-gather.2.cloned.1.call-start
  130.5 152.4 %reduce-scatter.2.cloned.1.call-done = bf16[2048,1024]{1,0:T(8,128)(2,1)} async-done(((bf16[8192,1024]{1,0:T(8,128)(2,1)}), bf16[2048,1024]{1,0:T(8,128)(2,1)}) %reduce-scatter.2.cloned.1.call-update) | async-done | bytes 4194320 | tf_op jit(solution)/shard_map/reduce_scatter | solution.py:97
  282.9 20.8 %abs_reduce_fusion.3 = (f32[2048]{0:T(1024)S(1)}, f32[1024]{0:T(1024)S(1)}, f32[1024]{0:T(1024)S(1)}, f32[2048]{0:T(1024)S(1)}, f32[2048,1024]{1,0:T(8,128)}, /*index=5*/bf16[2048,1024]{1,0:T(8,128)(2,1)}) fusion(bf16[2048,1024]{1,0:T(8,128)(2,1)} %reduce-scatter.2.cloned.1.call-done, f32[1024]{0:T(1024)S(1)} %copy-done.11, f32[2048]{0:T(1024)S(1)} %copy-done.7, ...), kind=kLoop, calls=%fused_computation.12 | loop fusion | flops 60811264 | bytes 33603584 | tf_op jit(solution)/shard_map/reduce_max | solution.py:117
  303.7 0.0 all-gather.2.cloned.1.call-update
  303.8 9.1 %pmax.15 = f32[2,1024]{1,0:T(2,128)S(1)} all-reduce(f32[2,1024]{1,0:T(2,128)S(1)} %pad_maximum_fusion.1), channel_id=1, replica_groups=mesh['dp'=4,'tensor'=8] {'dp'}, use_global_device_ids=true, to_apply=%region_9.10 | all-reduce | flops 2048 | bytes 16384 | tf_op jit(solution)/shard_map/pmax | solution.py:120
  312.9 26.3 %pmax.14 = f32[2,2048]{1,0:T(2,128)S(1)} all-reduce(f32[2,2048]{1,0:T(2,128)S(1)} %pad_maximum_fusion), channel_id=1, replica_groups=mesh['dp'=4,'tensor'=8] {'tensor'}, use_global_device_ids=true, to_apply=%region_6.7 | all-reduce | flops 4096 | bytes 32768 | tf_op jit(solution)/shard_map/pmax | solution.py:119
  339.2 0.0 copy-start.13
  339.3 0.0 copy-start.14
  339.3 11.0 %divide_convert_fusion = (bf16[2048,1024]{1,0:T(8,128)(2,1)}, bf16[2048,1024]{1,0:T(8,128)(2,1)}) fusion(f32[1024]{0:T(1024)S(1)} %bitcast.71, f32[2048]{0:T(1024)S(1)} %bitcast.65, bf16[2048,1024]{1,0:T(8,128)(2,1)} %reduce-scatter.2.cloned.1.call-done, f32[1024]{0:T(1024)S(1)} %copy-done.12, f32[2048]{0:T(1024)S(1)} %copy-done.8, ...), kind=kLoop, calls=%fused_computation.6 | loop fusion | flops 46137344 | bytes 21020672 | tf_op jit(solution)/shard_map/convert_element_type | solution.py:126
  350.4 110.8 %all-gather.2.cloned.1.call-done = bf16[8192,1024]{1,0:T(8,128)(2,1)} async-done(((bf16[2048,1024]{1,0:T(8,128)(2,1)}), bf16[8192,1024]{1,0:T(8,128)(2,1)}) %all-gather.2.cloned.1.call-update) | async-done | bytes 16777232 | tf_op jit(solution)/shard_map/all_gather | solution.py:93
  461.2 12.2 %fusion.24 = bf16[384,1024]{1,0:T(8,128)(2,1)S(1)} fusion(bf16[8192,1024]{1,0:T(8,128)(2,1)} %all-gather.2.cloned.1.call-done, bf16[384,16384]{1,0:T(8,128)(2,1)} %copy-done.6, s32[]{:T(128)S(6)} %select_n.29), kind=kOutput, calls=%fused_computation.34 | convolution fusion | flops 6442844160 | bytes 23855108 | tf_op jit(solution)/shard_map/dot_general | solution.py:91
  473.4 0.4 copy.30
  473.8 0.2 multiply_reduce_fusion
  474.0 3.6 multiply_convert_fusion
  477.7 1.2 copy.25
  (36 shorter events, 0.2 us)
Async XLA Ops:
  7.2 68.4 %copy-start = (bf16[384,1024]{1,0:T(8,128)(2,1)S(1)}, bf16[384,1024]{1,0:T(8,128)(2,1)}, u32[]{:S(2)}) copy-start(bf16[384,1024]{1,0:T(8,128)(2,1)} %param.12) | copy-start | bytes 2359300
  7.2 275.7 %reduce-scatter.2.cloned.1.call-start = ((), (), s32[]{:S(2)}) async-start(), calls=%async_computation.2 | async-start | bytes 20971520 | tf_op jit(solution)/shard_map/reduce_scatter | solution.py:97
  7.2 14.5 %collective-permute-start = (bf16[384,1024]{1,0:T(8,128)(2,1)}, bf16[384,1024]{1,0:T(8,128)(2,1)S(1)}, u32[]{:S(2)}, u32[]{:S(2)}) collective-permute-start(bf16[384,1024]{1,0:T(8,128)(2,1)} %param.14), channel_id=1, source_target_pairs={{0,1},{1,2},{2,3},{3,4},{4,5},{5,6},{6,7},{7,0},{8,9},{9,10},{10,1... | collective-permute-start | bytes 2359304 | tf_op jit(solution)/shard_map/ppermute | solution.py:80
  21.7 13.2 %collective-permute-start.1 = (bf16[384,1024]{1,0:T(8,128)(2,1)S(1)}, bf16[384,1024]{1,0:T(8,128)(2,1)S(1)}, u32[]{:S(2)}, u32[]{:S(2)}) collective-permute-start(bf16[384,1024]{1,0:T(8,128)(2,1)S(1)} %collective-permute-done), channel_id=1, source_target_pairs={{0,1},{1,2},{2,3},{3,4},{4,5},{5,6},{6,7},{7,0},{8,9},{9,10},{10,1... | collective-permute-start | bytes 2359304 | tf_op jit(solution)/shard_map/ppermute | solution.py:80
  34.9 13.2 %collective-permute-start.2 = (bf16[384,1024]{1,0:T(8,128)(2,1)S(1)}, bf16[384,1024]{1,0:T(8,128)(2,1)S(1)}, u32[]{:S(2)}, u32[]{:S(2)}) collective-permute-start(bf16[384,1024]{1,0:T(8,128)(2,1)S(1)} %collective-permute-done.1), channel_id=1, source_target_pairs={{0,1},{1,2},{2,3},{3,4},{4,5},{5,6},{6,7},{7,0},{8,9},{9,10},{10,1... | collective-permute-start | bytes 2359304 | tf_op jit(solution)/shard_map/ppermute | solution.py:80
  48.1 13.2 %collective-permute-start.3 = (bf16[384,1024]{1,0:T(8,128)(2,1)S(1)}, bf16[384,1024]{1,0:T(8,128)(2,1)S(1)}, u32[]{:S(2)}, u32[]{:S(2)}) collective-permute-start(bf16[384,1024]{1,0:T(8,128)(2,1)S(1)} %collective-permute-done.2), channel_id=1, source_target_pairs={{0,1},{1,2},{2,3},{3,4},{4,5},{5,6},{6,7},{7,0},{8,9},{9,10},{10,1... | collective-permute-start | bytes 2359304 | tf_op jit(solution)/shard_map/ppermute | solution.py:80
  61.3 0.9 copy-start.2
  62.2 13.3 %collective-permute-start.4 = (bf16[384,1024]{1,0:T(8,128)(2,1)S(1)}, bf16[384,1024]{1,0:T(8,128)(2,1)}, u32[]{:S(2)}, u32[]{:S(2)}) collective-permute-start(bf16[384,1024]{1,0:T(8,128)(2,1)S(1)} %collective-permute-done.3), channel_id=1, source_target_pairs={{0,1},{1,2},{2,3},{3,4},{4,5},{5,6},{6,7},{7,0},{8,9},{9,10},{10,1... | collective-permute-start | bytes 2359304 | tf_op jit(solution)/shard_map/ppermute | solution.py:80
  75.5 13.5 %collective-permute-start.5 = (bf16[384,1024]{1,0:T(8,128)(2,1)}, bf16[384,1024]{1,0:T(8,128)(2,1)}, u32[]{:S(2)}, u32[]{:S(2)}) collective-permute-start(bf16[384,1024]{1,0:T(8,128)(2,1)} %collective-permute-done.4), channel_id=1, source_target_pairs={{0,1},{1,2},{2,3},{3,4},{4,5},{5,6},{6,7},{7,0},{8,9},{9,10},{10,1... | collective-permute-start | bytes 2359304 | tf_op jit(solution)/shard_map/ppermute | solution.py:80
  89.1 13.5 %collective-permute-start.6 = (bf16[384,1024]{1,0:T(8,128)(2,1)}, bf16[384,1024]{1,0:T(8,128)(2,1)}, u32[]{:S(2)}, u32[]{:S(2)}) collective-permute-start(bf16[384,1024]{1,0:T(8,128)(2,1)} %collective-permute-done.5), channel_id=1, source_target_pairs={{0,1},{1,2},{2,3},{3,4},{4,5},{5,6},{6,7},{7,0},{8,9},{9,10},{10,1... | collective-permute-start | bytes 2359304 | tf_op jit(solution)/shard_map/ppermute | solution.py:80
  92.6 13.5 %copy-start.3 = (bf16[384,1024]{1,0:T(8,128)(2,1)S(1)}, bf16[384,1024]{1,0:T(8,128)(2,1)}, u32[]{:S(2)}) copy-start(bf16[384,1024]{1,0:T(8,128)(2,1)} %copy-done.2) | copy-start | bytes 2359300
  95.7 19.2 %copy-start.4 = (bf16[128,8,384]{2,0,1:T(8,128)(2,1)}, bf16[128,8,384]{2,0,1:T(8,128)(2,1)S(1)}, u32[]{:S(2)}) copy-start(bf16[128,8,384]{2,0,1:T(8,128)(2,1)S(1)} %fusion.21) | copy-start | bytes 2359300
  95.7 10.7 %copy-start.1 = (bf16[384,1024]{1,0:T(8,128)(2,1)S(1)}, bf16[384,1024]{1,0:T(8,128)(2,1)}, u32[]{:S(2)}) copy-start(bf16[384,1024]{1,0:T(8,128)(2,1)} %param.14) | copy-start | bytes 2359300
  110.4 4.5 copy-start.6
  130.2 152.6 %copy-start.7 = (f32[2048]{0:T(1024)S(1)}, f32[2048]{0:T(1024)}, u32[]{:S(2)}) copy-start(f32[2048]{0:T(1024)} %param.17) | copy-start | bytes 24580
  130.3 152.6 %copy-start.8 = (f32[2048]{0:T(1024)S(1)}, f32[2048]{0:T(1024)}, u32[]{:S(2)}) copy-start(f32[2048]{0:T(1024)} %param.20) | copy-start | bytes 24580
  130.3 152.6 %copy-start.11 = (f32[1024]{0:T(1024)S(1)}, f32[1024]{0:T(1024)}, u32[]{:S(2)}) copy-start(f32[1024]{0:T(1024)} %param.18) | copy-start | bytes 12292
  130.3 152.6 %copy-start.12 = (f32[1024]{0:T(1024)S(1)}, f32[1024]{0:T(1024)}, u32[]{:S(2)}) copy-start(f32[1024]{0:T(1024)} %param.21) | copy-start | bytes 12292
  130.3 330.9 %all-gather.2.cloned.1.call-start = ((), (), s32[]{:S(2)}) async-start(), calls=%async_computation.1 | async-start | bytes 20971520 | tf_op jit(solution)/shard_map/all_gather | solution.py:93
  339.2 11.1 %copy-start.13 = (f32[1,1024]{1,0:T(1,128)}, f32[1,1024]{1,0:T(1,128)S(1)}, u32[]{:S(2)}) copy-start(f32[1,1024]{1,0:T(1,128)S(1)} %get-tuple-element.28) | copy-start | bytes 12292
  339.3 11.1 %copy-start.14 = (f32[1,1024]{1,0:T(1,128)}, f32[1,1024]{1,0:T(1,128)S(1)}, u32[]{:S(2)}) copy-start(f32[1,1024]{1,0:T(1,128)S(1)} %get-tuple-element.29) | copy-start | bytes 12292
  339.3 11.0 %copy-start.9 = (f32[1,2048]{1,0:T(1,128)}, f32[1,2048]{1,0:T(1,128)S(1)}, u32[]{:S(2)}) copy-start(f32[1,2048]{1,0:T(1,128)S(1)} %get-tuple-element.26) | copy-start | bytes 24580
  339.3 11.0 %copy-start.10 = (f32[1,2048]{1,0:T(1,128)}, f32[1,2048]{1,0:T(1,128)S(1)}, u32[]{:S(2)}) copy-start(f32[1,2048]{1,0:T(1,128)S(1)} %get-tuple-element.27) | copy-start | bytes 24580
  350.3 123.4 %copy-start.5 = (bf16[128,8,384]{2,0,1:T(8,128)(2,1)S(1)}, bf16[128,8,384]{2,0,1:T(8,128)(2,1)}, u32[]{:S(2)}) copy-start(bf16[128,8,384]{2,0,1:T(8,128)(2,1)} %copy-done.4) | copy-start | bytes 2359300
Sparse Core Ops, SparseCore 0:
  130.4 152.4 reduce-scatter.1
  303.9 157.2 all-gather.1
